TPU v7x, 32 devices: a whole 2x2x4 slice. The times are simulated.
32 devices in a mesh: blk: 16 (over z, x, core), pair: 2 (over y).
Axes of the slice: x: 2, y: 2, z: 4, core: 2. Of those that a mesh axis runs over, the one named last changes fastest.
Arguments:
- vertex: bfloat16 [16, 2048, 2048], P('blk', 'pair'), may hold values from -0.125 to 0.125
- left_phase: bfloat16 [16, 2048, 512], P('blk', 'pair'), may hold values from -6 to 6
- right_phase: bfloat16 [16, 2048, 512], P('blk'), may hold values from -6 to 6
- tiles: bfloat16 [64, 512, 512], P('blk'), may hold values from -0.25 to 0.25
- orders: int32 [16], P('blk'), may hold values from 512 to 2048, as said below
- momentum: int32 [512], replicated, may hold values from 0 to 63
- frequency: int32 [512], replicated, may hold values from 0 to 31
Outputs:
- suscept: bfloat16 [64, 512, 512], P('blk', 'pair')
- sigma: float32 [2048], P(('blk', 'pair'))
Inputs may be any that keep to these rules, and one draw needn't show every extreme that they name: `orders`: every order is at least 512 and at most 2048; some walker has order exactly 2048.
All inputs are finite; a program needn't handle non-finite values.
Results may differ from a plain program's by a relative error of at most 0.0075.
Values may be sent and summed in bfloat16 or wider, within the bound.
A program may use at most 64 MiB of HBM per device.

v0:
```python
import math

import jax
import jax.numpy as jnp
from jax import lax
from jax.sharding import PartitionSpec as P

NMOM = 64
NFREQ = 32


def passed_along(value, axis, steps):
    count = lax.axis_size(axis)
    pairs = [(source, (source + steps) % count) for source in range(count)]
    return lax.ppermute(value, axis, pairs)


def transform_rows(vertex_rows, left_rows, right_full, live_rows, live_cols):
    masked = jnp.where(
        live_rows[:, None] & live_cols[None, :], vertex_rows, jnp.zeros_like(vertex_rows)
    )
    carried = jnp.dot(masked, right_full, preferred_element_type=jnp.float32).astype(jnp.bfloat16)
    return lax.dot_general(
        left_rows, carried, (((0,), (0,)), ((), ())), preferred_element_type=jnp.float32
    )


def per_device(vertex, left_phase, right_phase, tiles, orders, momentum, frequency):
    vertex_rows = vertex[0]
    left_rows = left_phase[0]
    right_full = right_phase[0]
    height = vertex_rows.shape[0]
    breadth = vertex_rows.shape[1]
    states = right_full.shape[1]
    member = lax.axis_index("pair")
    first_row = member * height
    order = orders[0]
    live_cols = jnp.arange(breadth, dtype=jnp.int32) < order
    row_ids = first_row + jnp.arange(height, dtype=jnp.int32)
    partial_value = transform_rows(vertex_rows, left_rows, right_full, row_ids < order, live_cols)
    scale = 1.0 / math.sqrt(breadth)
    own_half = (
        lax.psum_scatter(partial_value, "pair", scatter_dimension=0, tiled=True) * scale
    ).astype(jnp.bfloat16)
    green = lax.all_gather(own_half, "pair", axis=0, tiled=True)
    window = [green]
    moving = green
    for offset in range(2):
        moving = passed_along(moving, "blk", 1)
        window.append(moving)
    moving = green
    for offset in range(2):
        moving = passed_along(moving, "blk", -1)
        window.append(moving)
    half_states = states // 2
    first_state = member * half_states
    running = jnp.zeros((tiles.shape[0], half_states, states), jnp.float32)
    for walker_green in window:
        upper = lax.dynamic_slice_in_dim(walker_green, first_state, half_states, 0)
        inner = jnp.einsum("sa,tab->tsb", upper, tiles, preferred_element_type=jnp.float32).astype(
            jnp.bfloat16
        )
        running = running + jnp.einsum(
            "tsb,cb->tsc", inner, walker_green, preferred_element_type=jnp.float32
        )
    suscept = running * (1.0 / math.sqrt(states))
    summed = jnp.sum(suscept, axis=0)
    mom_rows = lax.dynamic_slice_in_dim(momentum, first_state, half_states, 0)
    onehot_mom = (mom_rows[:, None] == jnp.arange(NMOM, dtype=jnp.int32)[None, :]).astype(
        jnp.float32
    )
    onehot_freq = (frequency[:, None] == jnp.arange(NFREQ, dtype=jnp.int32)[None, :]).astype(
        jnp.float32
    )
    folded = jnp.dot(summed, onehot_freq, precision=lax.Precision.HIGHEST)
    cells = jnp.dot(onehot_mom.T, folded, precision=lax.Precision.HIGHEST)
    factor = 1.0 / math.sqrt(
        5.0 * tiles.shape[0] * lax.axis_size("blk") * states * states / (NMOM * NFREQ)
    )
    owned = lax.psum_scatter(
        (cells * factor).reshape(-1), ("blk", "pair"), scatter_dimension=0, tiled=True
    )
    return (suscept.astype(jnp.bfloat16), owned)


def solution(mesh):
    in_specs = (
        P("blk", "pair", None),
        P("blk", "pair", None),
        P("blk", None, None),
        P("blk", None, None),
        P("blk"),
        P(),
        P(),
    )
    out_specs = (P("blk", "pair", None), P(("blk", "pair")))
    return jax.shard_map(
        per_device, mesh=mesh, in_specs=in_specs, out_specs=out_specs, check_vma=False
    )
```

profile of v0, /device:TPU:0, one launch (start us, length us, event | category | flops | bytes accessed | tf_op | source)
XLA Modules:
  0.0 133.6 jit_solution(5243694163073652639)
XLA Ops:
  7.2 0.0 copy-start
  7.2 0.0 reduce-scatter.2.cloned.1.call-start
  8.0 7.0 %convolution_bitcast_fusion = f32[512,512]{0,1:T(8,128)} fusion(bf16[1,2048,512]{2,1,0:T(8,128)(2,1)} %param.9, bf16[1,1024,2048]{2,1,0:T(8,128)(2,1)} %param.7, pred[2048]{0:T(1024)(128)(4,1)S(1)} %iota_compare_fusion.4, pred[1024]{0:T(1024)(128)(4,1)S(1)} %add_compare_fusion, bf16[1,1024,512]{2,1,0:T(8,128)(2,1)} %param.8), kind=kOutput, calls=%fused_computation.23 | convolution fusion | flops 2689073152 | bytes 8391680 | tf_op jit(solution)/shard_map/dot_general | solution.py:23
  15.0 0.0 reduce-scatter.2.cloned.1.call-update
  15.0 23.3 %reduce-scatter.2.cloned.1.call-done = f32[256,512]{0,1:T(8,128)} async-done(((f32[512,512]{0,1:T(8,128)}), f32[256,512]{0,1:T(8,128)}) %reduce-scatter.2.cloned.1.call-update) | async-done | bytes 524304 | tf_op jit(solution)/shard_map/reduce_scatter | solution.py:43
  38.3 1.1 multiply_convert_fusion
  39.4 8.5 %all_gather.3 = bf16[512,512]{0,1:T(8,128)(2,1)S(1)} all-gather(bf16[256,512]{0,1:T(8,128)(2,1)S(1)} %multiply_convert_fusion), channel_id=1, replica_groups=mesh['blk'=16,'pair'=2] {'pair'}, dimensions={0}, use_global_device_ids=true | all-gather | bytes 786432 | tf_op jit(solution)/shard_map/all_gather | solution.py:45
  47.9 0.0 collective-permute-start
  47.9 4.4 %collective-permute-start.2 = (bf16[512,512]{0,1:T(8,128)(2,1)S(1)}, bf16[512,512]{0,1:T(8,128)(2,1)}, u32[]{:S(2)}, u32[]{:S(2)}) collective-permute-start(bf16[512,512]{0,1:T(8,128)(2,1)S(1)} %all_gather.3), channel_id=1, source_target_pairs={{0,30},{2,0},{4,2},{6,4},{8,6},{10,8},{12,10},{14,12},{16,14},{18,... | collective-permute-start | bytes 1572872 | tf_op jit(solution)/shard_map/ppermute | solution.py:15
  52.4 0.1 dynamic_slice.23
  52.4 2.6 %fusion.20 = f32[4,256,512]{2,1,0:T(8,128)} fusion(bf16[4,512,512]{2,1,0:T(8,128)(2,1)S(1)} %copy-done, bf16[512,512]{0,1:T(8,128)(2,1)S(1)} %all_gather.3, s32[]{:T(128)S(6)} %select_n.17), kind=kOutput, calls=%fused_computation.22 | convolution fusion | flops 1074266112 | bytes 4980740 | tf_op jit(solution)/shard_map/tsb,cb->tsc/dot_general | solution.py:63
  55.1 4.4 %collective-permute-done = bf16[512,512]{0,1:T(8,128)(2,1)} collective-permute-done((bf16[512,512]{0,1:T(8,128)(2,1)S(1)}, bf16[512,512]{0,1:T(8,128)(2,1)}, u32[]{:S(2)}, u32[]{:S(2)}) %collective-permute-start) | collective-permute-done | bytes 524320 | tf_op jit(solution)/shard_map/ppermute | solution.py:15
  59.4 1.8 %collective-permute-start.1 = (bf16[512,512]{0,1:T(8,128)(2,1)}, bf16[512,512]{0,1:T(8,128)(2,1)}, u32[]{:S(2)}, u32[]{:S(2)}) collective-permute-start(bf16[512,512]{0,1:T(8,128)(2,1)} %collective-permute-done), channel_id=1, source_target_pairs={{0,2},{2,4},{4,6},{6,8},{8,10},{10,12},{12,14},{14,16},{16,18},{18... | collective-permute-start | bytes 1572872 | tf_op jit(solution)/shard_map/ppermute | solution.py:15
  61.3 2.6 %collective-permute-start.3 = (bf16[512,512]{0,1:T(8,128)(2,1)}, bf16[512,512]{0,1:T(8,128)(2,1)S(1)}, u32[]{:S(2)}, u32[]{:S(2)}) collective-permute-start(bf16[512,512]{0,1:T(8,128)(2,1)} %collective-permute-done.2), channel_id=1, source_target_pairs={{0,30},{2,0},{4,2},{6,4},{8,6},{10,8},{12,10},{14,12},{16,14},{18,... | collective-permute-start | bytes 1572872 | tf_op jit(solution)/shard_map/ppermute | solution.py:15
  63.9 3.7 %fusion.17 = f32[4,256,512]{2,1,0:T(8,128)} fusion(bf16[4,512,512]{2,1,0:T(8,128)(2,1)S(1)} %copy-done, bf16[512,512]{0,1:T(8,128)(2,1)} %collective-permute-done.2, s32[]{:T(128)S(6)} %select_n.17), kind=kOutput, calls=%fused_computation.19 | convolution fusion | flops 1074266112 | bytes 4980740 | tf_op jit(solution)/shard_map/tsb,cb->tsc/dot_general | solution.py:63
  67.6 3.7 %fusion.19 = f32[4,256,512]{2,1,0:T(8,128)} fusion(bf16[4,512,512]{2,1,0:T(8,128)(2,1)S(1)} %copy-done, bf16[512,512]{0,1:T(8,128)(2,1)} %collective-permute-done, s32[]{:T(128)S(6)} %select_n.17), kind=kOutput, calls=%fused_computation.21 | convolution fusion | flops 1074266112 | bytes 4980740 | tf_op jit(solution)/shard_map/tsb,cb->tsc/dot_general | solution.py:63
  71.3 3.8 %fusion.18 = f32[4,256,512]{2,1,0:T(8,128)} fusion(bf16[4,512,512]{2,1,0:T(8,128)(2,1)S(1)} %copy-done, bf16[512,512]{0,1:T(8,128)(2,1)} %collective-permute-done.1, s32[]{:T(128)S(6)} %select_n.17), kind=kOutput, calls=%fused_computation.20 | convolution fusion | flops 1074266112 | bytes 4980740 | tf_op jit(solution)/shard_map/tsb,cb->tsc/dot_general | solution.py:63
  75.1 6.0 %fusion.66 = (f32[256,512]{1,0:T(8,128)S(1)}, bf16[4,256,512]{2,1,0:T(8,128)(2,1)}) fusion(bf16[512,512]{0,1:T(8,128)(2,1)S(1)} %collective-permute-done.3, bf16[4,512,512]{2,1,0:T(8,128)(2,1)S(1)} %copy-done, s32[]{:T(128)S(6)} %select_n.17, f32[4,256,512]{2,1,0:T(8,128)} %fusion.17, f32[4,256,512]{2,1,0:T(8,128)} %fusion.18, f32[4,256,512]{2,1,0:T(8,128)} %fusion.20, ...), kind=kOutput, calls=%fused_computation.55 | convolution fusion | flops 1077805056 | bytes 12845060 | tf_op jit(solution)/shard_map/tsb,cb->tsc/dot_general | solution.py:63
  81.1 0.4 fusion.51
  81.6 0.2 convolution_multiply_fusion
  81.8 0.1 copy.30
  81.9 0.1 reshape.62
  82.0 44.2 %all-reduce = f32[2048]{0:T(1024)S(1)} all-reduce(f32[2048]{0:T(1024)S(1)} %reshape.62), channel_id=3, replica_groups=mesh['blk'=16,'pair'=2] {'blk','pair'}, use_global_device_ids=true, to_apply=%region_2.3.clone | all-reduce | flops 2048 | bytes 16384
  126.1 0.6 dynamic-slice
  (10 shorter events, 0.0 us)
Async XLA Ops:
  7.2 45.3 %copy-start = (bf16[4,512,512]{2,1,0:T(8,128)(2,1)S(1)}, bf16[4,512,512]{2,1,0:T(8,128)(2,1)}, u32[]{:S(2)}) copy-start(bf16[4,512,512]{2,1,0:T(8,128)(2,1)} %param.10) | copy-start | bytes 6291460
  7.2 31.1 %reduce-scatter.2.cloned.1.call-start = ((), (), s32[]{:S(2)}) async-start(), calls=%async_computation.1 | async-start | bytes 1572864 | tf_op jit(solution)/shard_map/reduce_scatter | solution.py:43
  15.0 37.4 %copy-start.2 = (s32[512]{0:T(512)S(1)}, s32[512]{0:T(512)}, u32[]{:S(2)}) copy-start(s32[512]{0:T(512)} %param.12) | copy-start | bytes 6148
  47.9 11.5 %collective-permute-start = (bf16[512,512]{0,1:T(8,128)(2,1)S(1)}, bf16[512,512]{0,1:T(8,128)(2,1)}, u32[]{:S(2)}, u32[]{:S(2)}) collective-permute-start(bf16[512,512]{0,1:T(8,128)(2,1)S(1)} %all_gather.3), channel_id=1, source_target_pairs={{0,2},{2,4},{4,6},{6,8},{8,10},{10,12},{12,14},{14,16},{16,18},{18... | collective-permute-start | bytes 1572872 | tf_op jit(solution)/shard_map/ppermute | solution.py:15
  47.9 13.3 %collective-permute-start.2 = (bf16[512,512]{0,1:T(8,128)(2,1)S(1)}, bf16[512,512]{0,1:T(8,128)(2,1)}, u32[]{:S(2)}, u32[]{:S(2)}) collective-permute-start(bf16[512,512]{0,1:T(8,128)(2,1)S(1)} %all_gather.3), channel_id=1, source_target_pairs={{0,30},{2,0},{4,2},{6,4},{8,6},{10,8},{12,10},{14,12},{16,14},{18,... | collective-permute-start | bytes 1572872 | tf_op jit(solution)/shard_map/ppermute | solution.py:15
  59.4 11.9 %collective-permute-start.1 = (bf16[512,512]{0,1:T(8,128)(2,1)}, bf16[512,512]{0,1:T(8,128)(2,1)}, u32[]{:S(2)}, u32[]{:S(2)}) collective-permute-start(bf16[512,512]{0,1:T(8,128)(2,1)} %collective-permute-done), channel_id=1, source_target_pairs={{0,2},{2,4},{4,6},{6,8},{8,10},{10,12},{12,14},{14,16},{16,18},{18... | collective-permute-start | bytes 1572872 | tf_op jit(solution)/shard_map/ppermute | solution.py:15
  61.3 13.8 %collective-permute-start.3 = (bf16[512,512]{0,1:T(8,128)(2,1)}, bf16[512,512]{0,1:T(8,128)(2,1)S(1)}, u32[]{:S(2)}, u32[]{:S(2)}) collective-permute-start(bf16[512,512]{0,1:T(8,128)(2,1)} %collective-permute-done.2), channel_id=1, source_target_pairs={{0,30},{2,0},{4,2},{6,4},{8,6},{10,8},{12,10},{14,12},{16,14},{18,... | collective-permute-start | bytes 1572872 | tf_op jit(solution)/shard_map/ppermute | solution.py:15
  75.1 6.0 %copy-start.1 = (s32[512]{0:T(512)S(1)}, s32[512]{0:T(512)}, u32[]{:S(2)}) copy-start(s32[512]{0:T(512)} %param.13) | copy-start | bytes 6148
Sparse Core Ops, SparseCore 0:
  15.1 23.1 reduce-scatter.1
where the time goes:
time: 134 us
  blocking collectives  52.7 us (39%)
  waiting for transfers between devices  27.7 us (21%)
  matrix products  27.5 us (21%)
  between operations  14.9 us (11%)
  starting transfers between devices  8.92 us (7%)
    unnamed x1, blocking collectives  44.2 us
    reduce_scatter x1, waiting for transfers between devices, per_device(): lax.psum_scatter(partial_value, 'pair', scatter_dimension=0, tiled=True)  23.3 us
    dot_general x5, matrix products, per_device(): jnp.einsum('tsb,cb->tsc', inner, walker_green, preferred_element_type=jnp...  19.8 us
    ppermute x4, starting transfers between devices, passed_along(): return lax.ppermute(value, axis, pairs)  8.89 us
    all_gather x1, blocking collectives, per_device(): green = lax.all_gather(own_half, 'pair', axis=0, tiled=True)  8.53 us
    dot_general x1, matrix products, transform_rows(): lax.dot_general(left_rows, carried, (((0,), (0,)), ((), ())), preferred_e...  6.95 us
    ppermute x4, waiting for transfers between devices, passed_along(): return lax.ppermute(value, axis, pairs)  4.38 us
  transfers between devices with their start and end apart: 5, of which 2 were waited for; matrix products, arithmetic and copies ran while one was open for 10% of the time, Pallas kernels for 0%

commit v1 on v0

v1 whole, which is shorter than its diff:
```python
import math

import jax
import jax.numpy as jnp
from jax import lax
from jax.experimental import pallas as pl
from jax.experimental.pallas import tpu as pltpu
from jax.sharding import PartitionSpec as P

NMOM = 64
NFREQ = 32
LANES = 128
CHUNKS = 8
MESH = pl.DeviceIdType.MESH
OWN, PEER, ACROSS, RELAYED, FORWARDED = range(5)


def contract(a, b, dims, precision=None):
    return lax.dot_general(
        a, b, (dims, ((), ())), preferred_element_type=jnp.float32, precision=precision
    )


def body(sizes, order_ref, mom_ref, freq_ref, vertex_hbm, left_hbm, right_hbm, tiles_hbm,
         out_ref, sigma_ref,
         vertex, left, right, tiles, carried, partial, sending, arrived, greens, inner, acc,
         cells_ref, sig_send, sig_recv, load_sem, y_send, y_recv, x_send, x_recv, z_send, z_recv,
         p_send, p_recv, f_send, f_recv, s_send, s_recv):
    n_blk, n_pair, height, breadth, states, n_tiles = sizes
    count = n_blk * n_pair
    half = states // n_pair
    b = lax.axis_index("blk")
    p = lax.axis_index("pair")
    me = b * n_pair + p
    chip = b // 2
    core = lax.rem(b, 2)
    odd = lax.rem(chip, 2)
    step = 1 - 2 * odd
    across = (lax.rem(b + 2 * step + n_blk, n_blk), p)
    along = (lax.rem(b + 4 * step + n_blk, n_blk), p)
    peer = (b + 1 - 2 * core, p)
    other = (b, 1 - p)
    forwards_across = lax.rem(odd + core, 2) == 0

    barrier = pltpu.get_barrier_semaphore()

    def greet(i, carry):
        to = lax.rem(me + i, count)
        pl.semaphore_signal(barrier, inc=1, device_id=(to // n_pair, lax.rem(to, n_pair)),
                            device_id_type=MESH)
        return carry

    lax.fori_loop(1, count, greet, 0)

    pieces = 4
    block = height // pieces
    load_right = pltpu.make_async_copy(right_hbm.at[0], right, load_sem.at[0])
    load_right.start()
    load_vertex = []
    for i in range(pieces):
        rows = pl.ds(i * block, block)
        copy = pltpu.make_async_copy(vertex_hbm.at[0, rows], vertex.at[rows], load_sem.at[1 + i])
        copy.start()
        load_vertex.append(copy)
    load_left = pltpu.make_async_copy(left_hbm.at[0], left, load_sem.at[1 + pieces])
    load_left.start()
    load_tiles = pltpu.make_async_copy(tiles_hbm, tiles, load_sem.at[2 + pieces])
    load_tiles.start()

    order = order_ref[0]
    load_right.wait()

    def mask_right(i, carry):
        rows = pl.ds(pl.multiple_of(i * 256, 256), 256)
        ids = i * 256 + lax.broadcasted_iota(jnp.int32, (256, states), 0)
        right[rows, :] = jnp.where(ids < order, right[rows, :], jnp.zeros((), jnp.bfloat16))
        return carry

    lax.fori_loop(0, breadth // 256, mask_right, 0)

    for i in range(pieces):
        load_vertex[i].wait()
        rows = pl.ds(i * block, block)
        product = contract(vertex[rows, :], right[...], ((1,), (0,)))
        ids = p * height + i * block + lax.broadcasted_iota(jnp.int32, (block, states), 0)
        carried[rows, :] = jnp.where(ids < order, product, 0.0).astype(jnp.bfloat16)

    load_left.wait()
    pl.semaphore_wait(barrier, count - 1)

    scale = 1.0 / math.sqrt(breadth)
    size = states // CHUNKS
    per_half = half // size

    def chunk(which, k):
        return pl.ds(pl.multiple_of(lax.rem(which * per_half + k, CHUNKS) * size, size), size)

    def exchange(k):
        rows = chunk(1 - p, k)
        return pltpu.make_async_remote_copy(
            src_ref=sending.at[rows], dst_ref=arrived.at[rows], send_sem=y_send.at[k],
            recv_sem=y_recv.at[k], device_id=other, device_id_type=MESH)

    def arrival(k):
        rows = chunk(p, k)
        return pltpu.make_async_remote_copy(
            src_ref=sending.at[rows], dst_ref=arrived.at[rows], send_sem=y_send.at[k],
            recv_sem=y_recv.at[k], device_id=other, device_id_type=MESH)

    def hop(source, target, k, send, recv, device):
        rows = chunk(p, k)
        return pltpu.make_async_remote_copy(
            src_ref=greens.at[source, rows], dst_ref=greens.at[target, rows], send_sem=send.at[k],
            recv_sem=recv.at[k], device_id=device, device_id_type=MESH)

    def to_across(k):
        return hop(OWN, ACROSS, k, x_send, x_recv, across)

    def to_peer(k):
        return hop(OWN, PEER, k, p_send, p_recv, peer)

    def to_along(k):
        return hop(ACROSS, RELAYED, k, z_send, z_recv, along)

    def forward(source, k):
        return hop(source, FORWARDED, k, f_send, f_recv, peer)

    for part in range(n_pair):
        which = lax.rem(1 - p + part, n_pair)
        first = pl.multiple_of(which * half, half)
        rows = pl.ds(first, half)
        product = contract(left[:, rows], carried[...], ((0,), (0,))) * scale
        partial[rows, :] = product
        sending[rows, :] = product.astype(jnp.bfloat16)
        for k in range(per_half):
            exchange(part * per_half + k).start()

    ids_m = lax.broadcasted_iota(jnp.int32, (NMOM, half), 0)
    pick_mom = (ids_m == mom_ref[p]).astype(jnp.bfloat16)
    ids_f = lax.broadcasted_iota(jnp.int32, (LANES, states), 0)
    pick_freq = (ids_f == freq_ref[...]).astype(jnp.bfloat16)
    own_rows = pl.ds(pl.multiple_of(p * half, half), half)

    def compute_inner(slot, slot_index):
        upper = greens[slot, own_rows, :]
        total = jnp.zeros((half, states), jnp.float32)
        for t in range(n_tiles):
            value = contract(upper, tiles[t], ((1,), (0,))).astype(jnp.bfloat16)
            inner[slot_index, pl.ds(t * half, half), :] = value
            total = total + value.astype(jnp.float32)
        high = total.astype(jnp.bfloat16)
        low = (total - high.astype(jnp.float32)).astype(jnp.bfloat16)
        return contract(pick_mom, high, ((1,), (0,))) + contract(pick_mom, low, ((1,), (0,)))

    def compute_cells(slot, folded, first=False):
        picked = contract(pick_freq, greens[slot], ((1,), (0,)))
        value = contract(folded, picked, ((1,), (1,)), lax.Precision.HIGHEST)
        cells_ref[...] = value if first else cells_ref[...] + value

    out_scale = 1.0 / math.sqrt(states)

    def compute_chi(slot, slot_index, first=False, last=False):
        for t in range(n_tiles):
            rows = pl.ds(t * half, half)
            value = contract(inner[slot_index, rows, :], greens[slot], ((1,), (1,)))
            if not first:
                value = acc[rows, :] + value
            if last:
                out_ref[t] = (value * out_scale).astype(jnp.bfloat16)
            else:
                acc[rows, :] = value

    def take_y(k):
        arrival(k).wait_recv()
        rows = chunk(p, k)
        greens[OWN, rows, :] = (
            partial[rows, :] + arrived[rows, :].astype(jnp.float32)
        ).astype(jnp.bfloat16)
        to_across(k).start()
        to_peer(k).start()

    def take_x(k):
        to_across(k).wait_recv()
        to_along(k).start()

        @pl.when(forwards_across)
        def _():
            forward(ACROSS, k).start()

    def take_z(k):
        to_along(k).wait_recv()

        @pl.when(jnp.logical_not(forwards_across))
        def _():
            forward(RELAYED, k).start()

    folds = {}
    lag = 2
    for s in range(CHUNKS + 2 * lag):
        if s < CHUNKS:
            take_y(s)
        if 0 <= s - lag < CHUNKS:
            take_x(s - lag)
        if 0 <= s - 2 * lag < CHUNKS:
            take_z(s - 2 * lag)
        if s == per_half - 1:
            load_tiles.wait()
            folds[OWN] = compute_inner(OWN, 0)
        if s == per_half + 1:
            for k in range(per_half):
                to_peer(k).wait_recv()
            folds[PEER] = compute_inner(PEER, 1)
        if s == per_half + 2:
            folds[ACROSS] = compute_inner(ACROSS, 2)
        if s == CHUNKS - 1:
            compute_cells(OWN, folds[OWN], first=True)
            compute_chi(OWN, 0, first=True)
        if s == CHUNKS:
            folds[RELAYED] = compute_inner(RELAYED, 3)
        if s == CHUNKS + 1:
            for k in range(per_half, CHUNKS):
                to_peer(k).wait_recv()
            compute_cells(PEER, folds[PEER])
            compute_chi(PEER, 1)
        if s == CHUNKS + 2:
            for k in range(per_half):
                forward(ACROSS, k).wait_recv()
            folds[FORWARDED] = compute_inner(FORWARDED, 4)
            compute_cells(ACROSS, folds[ACROSS])

    compute_cells(RELAYED, folds[RELAYED])
    for k in range(per_half, CHUNKS):
        forward(ACROSS, k).wait_recv()
    compute_cells(FORWARDED, folds[FORWARDED])

    own_cells = NMOM * NFREQ // count
    cells = cells_ref[...]
    rows_d = lax.broadcasted_iota(jnp.int32, (count, NMOM), 0)
    cols_m = lax.broadcasted_iota(jnp.int32, (count, NMOM), 1)
    spread = jnp.zeros((count, LANES), jnp.float32)
    if own_cells >= NFREQ:
        group = own_cells // NFREQ
        for k in range(group):
            pick = (cols_m == rows_d * group + k).astype(jnp.float32)
            value = contract(pick, cells, ((1,), (0,)), lax.Precision.HIGHEST)
            spread = spread + (pltpu.roll(value, NFREQ * k, 1) if k else value)
    else:
        group = NFREQ // own_cells
        for k in range(group):
            pick = (rows_d == cols_m * group + k).astype(jnp.float32)
            value = contract(pick, cells, ((1,), (0,)), lax.Precision.HIGHEST)
            spread = spread + (pltpu.roll(value, LANES - own_cells * k, 1) if k else value)
    factor = 1.0 / math.sqrt(5.0 * n_tiles * n_blk * states * states / (NMOM * NFREQ))
    spread = spread * (factor * out_scale)
    sig_send[...] = spread.reshape(count, 1, LANES)

    def owner(i):
        to = lax.rem(me + i, count)
        return pltpu.make_async_remote_copy(
            src_ref=sig_send.at[to], dst_ref=sig_recv.at[i - 1], send_sem=s_send.at[i - 1],
            recv_sem=s_recv.at[i - 1], device_id=(to // n_pair, lax.rem(to, n_pair)),
            device_id_type=MESH)

    def send_cells(i, carry):
        owner(i).start()
        return carry

    lax.fori_loop(1, count, send_cells, 0)

    compute_chi(ACROSS, 2)
    compute_chi(RELAYED, 3)
    compute_chi(FORWARDED, 4, last=True)

    for k in range(CHUNKS):
        exchange(k).wait_send()
        to_across(k).wait_send()
        to_peer(k).wait_send()
        to_along(k).wait_send()
        forward(ACROSS, k).wait_send()

    def take_cells(i, carry):
        owner(i).wait()
        return carry

    lax.fori_loop(1, count, take_cells, 0)
    sigma_ref[...] = jnp.sum(sig_recv[...], axis=0) + sig_send[me]


def solution(mesh):
    n_blk, n_pair = mesh.shape["blk"], mesh.shape["pair"]
    count = n_blk * n_pair

    def per_device(vertex, left_phase, right_phase, tiles, orders, momentum, frequency):
        height, breadth = vertex.shape[1], vertex.shape[2]
        states = right_phase.shape[2]
        n_tiles = tiles.shape[0]
        half = states // n_pair
        sizes = (n_blk, n_pair, height, breadth, states, n_tiles)
        bf16, f32 = jnp.bfloat16, jnp.float32
        dma = pltpu.SemaphoreType.DMA
        chi, cells = pl.pallas_call(
            lambda *refs: body(sizes, *refs),
            out_shape=(
                jax.ShapeDtypeStruct((n_tiles, half, states), bf16),
                jax.ShapeDtypeStruct((1, LANES), f32),
            ),
            in_specs=[
                pl.BlockSpec(memory_space=pltpu.SMEM),
                pl.BlockSpec(memory_space=pltpu.VMEM),
                pl.BlockSpec(memory_space=pltpu.VMEM),
            ] + [pl.BlockSpec(memory_space=pl.ANY)] * 4,
            out_specs=(
                pl.BlockSpec(memory_space=pltpu.VMEM),
                pl.BlockSpec(memory_space=pltpu.VMEM),
            ),
            scratch_shapes=[
                pltpu.VMEM((height, breadth), bf16),
                pltpu.VMEM((height, states), bf16),
                pltpu.VMEM((breadth, states), bf16),
                pltpu.VMEM((n_tiles, states, states), bf16),
                pltpu.VMEM((height, states), bf16),
                pltpu.VMEM((states, states), f32),
                pltpu.VMEM((states, states), bf16),
                pltpu.VMEM((states, states), bf16),
                pltpu.VMEM((5, states, states), bf16),
                pltpu.VMEM((5, n_tiles * half, states), bf16),
                pltpu.VMEM((n_tiles * half, states), f32),
                pltpu.VMEM((NMOM, LANES), f32),
                pltpu.VMEM((count, 1, LANES), f32),
                pltpu.VMEM((count - 1, 1, LANES), f32),
                dma((7,)),
            ] + [dma((CHUNKS,))] * 10 + [dma((count - 1,))] * 2,
            compiler_params=pltpu.CompilerParams(
                collective_id=0, has_side_effects=True, vmem_limit_bytes=60 * 1024 * 1024
            ),
            name="measure_green",
        )(
            orders,
            momentum.reshape(n_pair, 1, half),
            frequency.reshape(1, states),
            vertex,
            left_phase,
            right_phase,
            tiles,
        )
        own = NMOM * NFREQ // count
        return chi, cells[0, :own]

    in_specs = (
        P("blk", "pair", None),
        P("blk", "pair", None),
        P("blk", None, None),
        P("blk", None, None),
        P("blk"),
        P(),
        P(),
    )
    out_specs = (P("blk", "pair", None), P(("blk", "pair")))
    return jax.shard_map(
        per_device, mesh=mesh, in_specs=in_specs, out_specs=out_specs, check_vma=False
    )
```

time: 134 us -> 46.7 us (0.35)
  blocking collectives: 52.7 us -> 0 us
  Pallas kernels: 0 us -> 41.8 us
  waiting for transfers between devices: 27.7 us -> 0 us
  matrix products: 27.5 us -> 0 us
  between operations: 14.9 us -> 1.29 us
  starting transfers between devices: 8.92 us -> 0 us
  local copies, waits for them, and re-layouts: 0.84 us -> 3.38 us
    unnamed x1 -> x0, blocking collectives: 44.2 us -> none
    pallas_call x0 -> x1, Pallas kernels: none -> 41.8 us  [per_device(): pl.pallas_call(lambda *refs: body(sizes, *refs), out_shape=(jax.ShapeDtyp...]
    dot_general x8 -> x0, matrix products: 27.5 us -> none  [the longest x5 19.8 us: per_device(): jnp.einsum('tsb,cb->tsc', inner, walker_green, preferred_element_type=jnp...]
    reduce_scatter x1 -> x0, waiting for transfers between devices: 23.3 us -> none  [per_device(): lax.psum_scatter(partial_value, 'pair', scatter_dimension=0, tiled=True)]
    ppermute x4 -> x0, starting transfers between devices: 8.89 us -> none  [passed_along(): return lax.ppermute(value, axis, pairs)]
    all_gather x1 -> x0, blocking collectives: 8.53 us -> none  [per_device(): green = lax.all_gather(own_half, 'pair', axis=0, tiled=True)]
    ppermute x4 -> x0, waiting for transfers between devices: 4.38 us -> none  [passed_along(): return lax.ppermute(value, axis, pairs)]
    unnamed x7 -> x1, local copies, waits for them, and re-layouts: 0.6 us -> 2.26 us
  transfers between devices with their start and end apart: 5 -> 0, of which waited for: 2 -> 0; matrix products, arithmetic and copies ran while one was open for 10% -> 0% of each run, Pallas kernels for 0% -> 0%
where the time goes in v1:
time: 46.7 us; the launch traced here: 46.5 us
  Pallas kernels  41.8 us (90%)
  local copies, waits for them, and re-layouts  3.38 us (7%)
  between operations  1.29 us (3%)
    pallas_call x1, Pallas kernels, per_device(): pl.pallas_call(lambda *refs: body(sizes, *refs), out_shape=(jax.ShapeDtyp...  41.8 us
    unnamed x1, local copies, waits for them, and re-layouts  2.26 us
    squeeze x1, local copies, waits for them, and re-layouts, per_device(): return (chi, cells[0, :own])  1.11 us

profile of v1, /device:TPU:0, one launch (start us, length us, event | category | flops | bytes accessed | tf_op | source)
XLA Modules:
  0.0 46.5 jit_solution(2496409034750277921)
XLA Ops:
  1.3 41.8 %measure_green.1 = (bf16[4,256,512]{2,1,0:T(8,128)(2,1)}, f32[1,128]{1,0:T(1,128)}) custom-call(s32[1]{0:T(128)S(6)} %copy.10.refs_0_, s32[2,1,256]{2,1,0:T(1,128)} %bitcast.4, s32[1,512]{1,0:T(1,128)} %bitcast.5, bf16[1,1024,2048]{2,1,0:T(8,128)(2,1)} %refs_3_.1, bf16[1,1024,512]{2,1,0:T(8,128)(2,1)} %refs_4_.1, bf16[1,2048,512]{2,1,0:T(8,128)(2,1)} %refs_5_.1, ...), custom_call_target="tpu_custom_call" | custom-call | tf_op jit(solution)/shard_map/measure_green/pallas_call | solution.py:301
  43.1 1.1 %slice_bitcast_fusion = f32[64]{0:T(128)} fusion(f32[1,128]{1,0:T(1,128)} %get-tuple-element.5), kind=kLoop, calls=%fused_computation | loop fusion | bytes 512 | tf_op jit(solution)/shard_map/squeeze | solution.py:347
  44.2 2.3 %copy.11 = bf16[4,256,512]{2,1,0:T(8,128)(2,1)} copy(bf16[4,256,512]{2,1,0:T(8,128)(2,1)} %get-tuple-element.8) | data formatting | bytes 2097152

commit v2 on v1

--- a/solution.py
+++ b/solution.py
@@ -11,6 +11,7 @@
 NFREQ = 32
 LANES = 128
 CHUNKS = 8
+SPLIT = 2
 MESH = pl.DeviceIdType.MESH
 OWN, PEER, ACROSS, RELAYED, FORWARDED = range(5)
 
@@ -25,7 +26,8 @@
          out_ref, sigma_ref,
          vertex, left, right, tiles, carried, partial, sending, arrived, greens, inner, acc,
          cells_ref, sig_send, sig_recv, load_sem, y_send, y_recv, x_send, x_recv, z_send, z_recv,
-         p_send, p_recv, f_send, f_recv, s_send, s_recv):
+         p_send, p_recv, f_send, f_recv, s_send, s_recv,
+         chi, o_sem):
     n_blk, n_pair, height, breadth, states, n_tiles = sizes
     count = n_blk * n_pair
     half = states // n_pair
@@ -54,63 +56,53 @@
 
     pieces = 4
     block = height // pieces
-    load_right = pltpu.make_async_copy(right_hbm.at[0], right, load_sem.at[0])
-    load_right.start()
+    wide = states // SPLIT
+
+    def load_right(h):
+        cols = pl.ds(h * wide, wide)
+        return pltpu.make_async_copy(right_hbm.at[0, :, cols], right.at[h], load_sem.at[h])
+
+    load_right(0).start()
     load_vertex = []
     for i in range(pieces):
         rows = pl.ds(i * block, block)
-        copy = pltpu.make_async_copy(vertex_hbm.at[0, rows], vertex.at[rows], load_sem.at[1 + i])
+        copy = pltpu.make_async_copy(vertex_hbm.at[0, rows], vertex.at[rows], load_sem.at[SPLIT + i])
         copy.start()
         load_vertex.append(copy)
-    load_left = pltpu.make_async_copy(left_hbm.at[0], left, load_sem.at[1 + pieces])
+    load_left = pltpu.make_async_copy(left_hbm.at[0], left, load_sem.at[SPLIT + pieces])
     load_left.start()
-    load_tiles = pltpu.make_async_copy(tiles_hbm, tiles, load_sem.at[2 + pieces])
+    for h in range(1, SPLIT):
+        load_right(h).start()
+    load_tiles = pltpu.make_async_copy(tiles_hbm, tiles, load_sem.at[SPLIT + 1 + pieces])
     load_tiles.start()
 
     order = order_ref[0]
-    load_right.wait()
-
-    def mask_right(i, carry):
-        rows = pl.ds(pl.multiple_of(i * 256, 256), 256)
-        ids = i * 256 + lax.broadcasted_iota(jnp.int32, (256, states), 0)
-        right[rows, :] = jnp.where(ids < order, right[rows, :], jnp.zeros((), jnp.bfloat16))
-        return carry
-
-    lax.fori_loop(0, breadth // 256, mask_right, 0)
-
-    for i in range(pieces):
-        load_vertex[i].wait()
-        rows = pl.ds(i * block, block)
-        product = contract(vertex[rows, :], right[...], ((1,), (0,)))
-        ids = p * height + i * block + lax.broadcasted_iota(jnp.int32, (block, states), 0)
-        carried[rows, :] = jnp.where(ids < order, product, 0.0).astype(jnp.bfloat16)
-
-    load_left.wait()
-    pl.semaphore_wait(barrier, count - 1)
-
     scale = 1.0 / math.sqrt(breadth)
-    size = states // CHUNKS
+    per_split = CHUNKS // SPLIT
+    size = states // per_split
     per_half = half // size
 
     def chunk(which, k):
-        return pl.ds(pl.multiple_of(lax.rem(which * per_half + k, CHUNKS) * size, size), size)
+        index = lax.rem(which * per_half + k % per_split, per_split)
+        return (pl.ds(pl.multiple_of(index * size, size), size),
+                pl.ds(k // per_split * wide, wide))
 
     def exchange(k):
         rows = chunk(1 - p, k)
         return pltpu.make_async_remote_copy(
-            src_ref=sending.at[rows], dst_ref=arrived.at[rows], send_sem=y_send.at[k],
+            src_ref=sending.at[*rows], dst_ref=arrived.at[*rows], send_sem=y_send.at[k],
             recv_sem=y_recv.at[k], device_id=other, device_id_type=MESH)
 
     def arrival(k):
         rows = chunk(p, k)
         return pltpu.make_async_remote_copy(
-            src_ref=sending.at[rows], dst_ref=arrived.at[rows], send_sem=y_send.at[k],
+            src_ref=sending.at[*rows], dst_ref=arrived.at[*rows], send_sem=y_send.at[k],
             recv_sem=y_recv.at[k], device_id=other, device_id_type=MESH)
 
     def hop(source, target, k, send, recv, device):
         rows = chunk(p, k)
         return pltpu.make_async_remote_copy(
-            src_ref=greens.at[source, rows], dst_ref=greens.at[target, rows], send_sem=send.at[k],
+            src_ref=greens.at[source, *rows], dst_ref=greens.at[target, *rows], send_sem=send.at[k],
             recv_sem=recv.at[k], device_id=device, device_id_type=MESH)
 
     def to_across(k):
@@ -125,15 +117,35 @@
     def forward(source, k):
         return hop(source, FORWARDED, k, f_send, f_recv, peer)
 
-    for part in range(n_pair):
-        which = lax.rem(1 - p + part, n_pair)
-        first = pl.multiple_of(which * half, half)
-        rows = pl.ds(first, half)
-        product = contract(left[:, rows], carried[...], ((0,), (0,))) * scale
-        partial[rows, :] = product
-        sending[rows, :] = product.astype(jnp.bfloat16)
-        for k in range(per_half):
-            exchange(part * per_half + k).start()
+    for h in range(SPLIT):
+        load_right(h).wait()
+
+        def mask_right(i, carry):
+            rows = pl.ds(pl.multiple_of(i * 256, 256), 256)
+            ids = i * 256 + lax.broadcasted_iota(jnp.int32, (256, wide), 0)
+            right[h, rows, :] = jnp.where(ids < order, right[h, rows, :], jnp.zeros((), jnp.bfloat16))
+            return carry
+
+        lax.fori_loop(0, breadth // 256, mask_right, 0)
+        for i in range(pieces):
+            rows = pl.ds(i * block, block)
+            if h == 0:
+                load_vertex[i].wait()
+            product = contract(vertex[rows, :], right[h], ((1,), (0,)))
+            ids = p * height + i * block + lax.broadcasted_iota(jnp.int32, (block, wide), 0)
+            carried[rows, :] = jnp.where(ids < order, product, 0.0).astype(jnp.bfloat16)
+        if h == 0:
+            load_left.wait()
+            pl.semaphore_wait(barrier, count - 1)
+        cols = pl.ds(h * wide, wide)
+        for part in range(n_pair):
+            which = lax.rem(1 - p + part, n_pair)
+            rows = pl.ds(pl.multiple_of(which * half, half), half)
+            product = contract(left[:, rows], carried[...], ((0,), (0,))) * scale
+            partial[rows, cols] = product
+            sending[rows, cols] = product.astype(jnp.bfloat16)
+            for k in range(per_half):
+                exchange(h * per_split + part * per_half + k).start()
 
     ids_m = lax.broadcasted_iota(jnp.int32, (NMOM, half), 0)
     pick_mom = (ids_m == mom_ref[p]).astype(jnp.bfloat16)
@@ -159,6 +171,9 @@
 
     out_scale = 1.0 / math.sqrt(states)
 
+    def store(t):
+        return pltpu.make_async_copy(chi.at[t], out_ref.at[t], o_sem.at[t])
+
     def compute_chi(slot, slot_index, first=False, last=False):
         for t in range(n_tiles):
             rows = pl.ds(t * half, half)
@@ -166,15 +181,16 @@
             if not first:
                 value = acc[rows, :] + value
             if last:
-                out_ref[t] = (value * out_scale).astype(jnp.bfloat16)
+                chi[t] = (value * out_scale).astype(jnp.bfloat16)
+                store(t).start()
             else:
                 acc[rows, :] = value
 
     def take_y(k):
         arrival(k).wait_recv()
         rows = chunk(p, k)
-        greens[OWN, rows, :] = (
-            partial[rows, :] + arrived[rows, :].astype(jnp.float32)
+        greens[OWN, *rows] = (
+            partial[*rows] + arrived[*rows].astype(jnp.float32)
         ).astype(jnp.bfloat16)
         to_across(k).start()
         to_peer(k).start()
@@ -195,6 +211,7 @@
             forward(RELAYED, k).start()
 
     folds = {}
+    upper_last = CHUNKS - per_split + per_half - 1
     lag = 2
     for s in range(CHUNKS + 2 * lag):
         if s < CHUNKS:
@@ -203,33 +220,28 @@
             take_x(s - lag)
         if 0 <= s - 2 * lag < CHUNKS:
             take_z(s - 2 * lag)
-        if s == per_half - 1:
+        if s == upper_last:
             load_tiles.wait()
             folds[OWN] = compute_inner(OWN, 0)
-        if s == per_half + 1:
-            for k in range(per_half):
-                to_peer(k).wait_recv()
-            folds[PEER] = compute_inner(PEER, 1)
-        if s == per_half + 2:
-            folds[ACROSS] = compute_inner(ACROSS, 2)
         if s == CHUNKS - 1:
             compute_cells(OWN, folds[OWN], first=True)
             compute_chi(OWN, 0, first=True)
         if s == CHUNKS:
+            for k in range(CHUNKS):
+                to_peer(k).wait_recv()
+            folds[PEER] = compute_inner(PEER, 1)
+            folds[ACROSS] = compute_inner(ACROSS, 2)
+        if s == CHUNKS + 1:
+            compute_cells(PEER, folds[PEER])
+            compute_cells(ACROSS, folds[ACROSS])
+        if s == CHUNKS + lag:
             folds[RELAYED] = compute_inner(RELAYED, 3)
-        if s == CHUNKS + 1:
-            for k in range(per_half, CHUNKS):
-                to_peer(k).wait_recv()
-            compute_cells(PEER, folds[PEER])
-            compute_chi(PEER, 1)
-        if s == CHUNKS + 2:
-            for k in range(per_half):
+            for k in range(upper_last + 1):
                 forward(ACROSS, k).wait_recv()
             folds[FORWARDED] = compute_inner(FORWARDED, 4)
-            compute_cells(ACROSS, folds[ACROSS])
 
     compute_cells(RELAYED, folds[RELAYED])
-    for k in range(per_half, CHUNKS):
+    for k in range(upper_last + 1, CHUNKS):
         forward(ACROSS, k).wait_recv()
     compute_cells(FORWARDED, folds[FORWARDED])
 
@@ -267,6 +279,7 @@
 
     lax.fori_loop(1, count, send_cells, 0)
 
+    compute_chi(PEER, 1)
     compute_chi(ACROSS, 2)
     compute_chi(RELAYED, 3)
     compute_chi(FORWARDED, 4, last=True)
@@ -277,6 +290,9 @@
         to_peer(k).wait_send()
         to_along(k).wait_send()
         forward(ACROSS, k).wait_send()
+
+    for t in range(n_tiles):
+        store(t).wait()
 
     def take_cells(i, carry):
         owner(i).wait()
@@ -308,17 +324,17 @@
                 pl.BlockSpec(memory_space=pltpu.SMEM),
                 pl.BlockSpec(memory_space=pltpu.VMEM),
                 pl.BlockSpec(memory_space=pltpu.VMEM),
-            ] + [pl.BlockSpec(memory_space=pl.ANY)] * 4,
+            ] + [pl.BlockSpec(memory_space=pltpu.HBM)] * 4,
             out_specs=(
-                pl.BlockSpec(memory_space=pltpu.VMEM),
+                pl.BlockSpec(memory_space=pltpu.HBM),
                 pl.BlockSpec(memory_space=pltpu.VMEM),
             ),
             scratch_shapes=[
                 pltpu.VMEM((height, breadth), bf16),
                 pltpu.VMEM((height, states), bf16),
-                pltpu.VMEM((breadth, states), bf16),
+                pltpu.VMEM((SPLIT, breadth, states // SPLIT), bf16),
                 pltpu.VMEM((n_tiles, states, states), bf16),
-                pltpu.VMEM((height, states), bf16),
+                pltpu.VMEM((height, states // SPLIT), bf16),
                 pltpu.VMEM((states, states), f32),
                 pltpu.VMEM((states, states), bf16),
                 pltpu.VMEM((states, states), bf16),
@@ -328,8 +344,9 @@
                 pltpu.VMEM((NMOM, LANES), f32),
                 pltpu.VMEM((count, 1, LANES), f32),
                 pltpu.VMEM((count - 1, 1, LANES), f32),
-                dma((7,)),
-            ] + [dma((CHUNKS,))] * 10 + [dma((count - 1,))] * 2,
+                dma((SPLIT + 6,)),
+            ] + [dma((CHUNKS,))] * 10 + [dma((count - 1,))] * 2 + [
+                pltpu.VMEM((n_tiles, half, states), bf16), dma((n_tiles,))],
             compiler_params=pltpu.CompilerParams(
                 collective_id=0, has_side_effects=True, vmem_limit_bytes=60 * 1024 * 1024
             ),

time: 46.7 us -> 46.4 us (level)
  no operation moved by 1% of the time
where the time goes in v2:
time: 46.4 us; the launch traced here: 46.2 us
  Pallas kernels  41.5 us (89%)
  local copies, waits for them, and re-layouts  3.38 us (7%)
  between operations  1.29 us (3%)
    pallas_call x1, Pallas kernels, per_device(): pl.pallas_call(lambda *refs: body(sizes, *refs), out_shape=(jax.ShapeDtyp...  41.5 us
    unnamed x1, local copies, waits for them, and re-layouts  2.26 us
    squeeze x1, local copies, waits for them, and re-layouts, per_device(): return (chi, cells[0, :own])  1.11 us

profile of v2, /device:TPU:0, one launch (start us, length us, event | category | flops | bytes accessed | tf_op | source)
XLA Modules:
  0.0 46.2 jit_solution(5258899396836246910)
XLA Ops:
  1.3 41.5 %measure_green.1 = (bf16[4,256,512]{2,1,0:T(8,128)(2,1)}, f32[1,128]{1,0:T(1,128)}) custom-call(s32[1]{0:T(128)S(6)} %copy.10.refs_0_, s32[2,1,256]{2,1,0:T(1,128)} %bitcast.4, s32[1,512]{1,0:T(1,128)} %bitcast.5, bf16[1,1024,2048]{2,1,0:T(8,128)(2,1)} %refs_3_.1, bf16[1,1024,512]{2,1,0:T(8,128)(2,1)} %refs_4_.1, bf16[1,2048,512]{2,1,0:T(8,128)(2,1)} %refs_5_.1, ...), custom_call_target="tpu_custom_call" | custom-call | tf_op jit(solution)/shard_map/measure_green/pallas_call | solution.py:317
  42.8 1.1 %slice_bitcast_fusion = f32[64]{0:T(128)} fusion(f32[1,128]{1,0:T(1,128)} %get-tuple-element.5), kind=kLoop, calls=%fused_computation | loop fusion | bytes 512 | tf_op jit(solution)/shard_map/squeeze | solution.py:364
  43.9 2.3 %copy.11 = bf16[4,256,512]{2,1,0:T(8,128)(2,1)} copy(bf16[4,256,512]{2,1,0:T(8,128)(2,1)} %get-tuple-element.8) | data formatting | bytes 2097152

commit v3 on v2

--- a/solution.py
+++ b/solution.py
@@ -10,7 +10,7 @@
 NMOM = 64
 NFREQ = 32
 LANES = 128
-CHUNKS = 8
+CHUNKS = 4
 SPLIT = 2
 MESH = pl.DeviceIdType.MESH
 OWN, PEER, ACROSS, RELAYED, FORWARDED = range(5)
@@ -234,6 +234,7 @@
         if s == CHUNKS + 1:
             compute_cells(PEER, folds[PEER])
             compute_cells(ACROSS, folds[ACROSS])
+            compute_chi(PEER, 1)
         if s == CHUNKS + lag:
             folds[RELAYED] = compute_inner(RELAYED, 3)
             for k in range(upper_last + 1):
@@ -279,7 +280,6 @@
 
     lax.fori_loop(1, count, send_cells, 0)
 
-    compute_chi(PEER, 1)
     compute_chi(ACROSS, 2)
     compute_chi(RELAYED, 3)
     compute_chi(FORWARDED, 4, last=True)
@@ -299,7 +299,8 @@
         return carry
 
     lax.fori_loop(1, count, take_cells, 0)
-    sigma_ref[...] = jnp.sum(sig_recv[...], axis=0) + sig_send[me]
+    total = jnp.sum(sig_recv[...], axis=0) + sig_send[me]
+    sigma_ref[...] = total[:, :own_cells]
 
 
 def solution(mesh):
@@ -318,7 +319,7 @@
             lambda *refs: body(sizes, *refs),
             out_shape=(
                 jax.ShapeDtypeStruct((n_tiles, half, states), bf16),
-                jax.ShapeDtypeStruct((1, LANES), f32),
+                jax.ShapeDtypeStruct((1, NMOM * NFREQ // count), f32),
             ),
             in_specs=[
                 pl.BlockSpec(memory_space=pltpu.SMEM),
@@ -360,8 +361,7 @@
             right_phase,
             tiles,
         )
-        own = NMOM * NFREQ // count
-        return chi, cells[0, :own]
+        return chi, cells.reshape(-1)
 
     in_specs = (
         P("blk", "pair", None),

time: 46.4 us -> 45.3 us (0.976)
  local copies, waits for them, and re-layouts: 3.38 us -> 2.78 us
  Pallas kernels: 41.5 us -> 41 us
    squeeze x1 -> x0, local copies, waits for them, and re-layouts: 1.11 us -> none  [per_device(): return (chi, cells[0, :own])]
    pallas_call x1, Pallas kernels: 41.5 us -> 41 us  [per_device(): pl.pallas_call(lambda *refs: body(sizes, *refs), out_shape=(jax.ShapeDtyp...]
    unnamed x1 -> x4, local copies, waits for them, and re-layouts: 2.26 us -> 2.78 us
where the time goes in v3:
time: 45.3 us; the launch traced here: 45.1 us
  Pallas kernels  41 us (91%)
  local copies, waits for them, and re-layouts  2.78 us (6%)
  between operations  1.29 us (3%)
    pallas_call x1, Pallas kernels, per_device(): pl.pallas_call(lambda *refs: body(sizes, *refs), out_shape=(jax.ShapeDtyp...  41 us
    unnamed x4, local copies, waits for them, and re-layouts  2.78 us

profile of v3, /device:TPU:0, one launch (start us, length us, event | category | flops | bytes accessed | tf_op | source)
XLA Modules:
  0.0 45.1 jit_solution(5502356341065239709)
XLA Ops:
  1.3 41.0 %measure_green.1 = (bf16[4,256,512]{2,1,0:T(8,128)(2,1)}, f32[1,64]{1,0:T(1,128)}) custom-call(s32[1]{0:T(128)S(6)} %copy.11.refs_0_, s32[2,1,256]{2,1,0:T(1,128)} %bitcast.3, s32[1,512]{1,0:T(1,128)} %bitcast.4, bf16[1,1024,2048]{2,1,0:T(8,128)(2,1)} %refs_3_.1, bf16[1,1024,512]{2,1,0:T(8,128)(2,1)} %refs_4_.1, bf16[1,2048,512]{2,1,0:T(8,128)(2,1)} %refs_5_.1, ...), custom_call_target="tpu_custom_call" | custom-call | tf_op jit(solution)/shard_map/measure_green/pallas_call | solution.py:318
  42.3 0.0 copy-start
  42.3 2.3 %copy.12 = bf16[4,256,512]{2,1,0:T(8,128)(2,1)} copy(bf16[4,256,512]{2,1,0:T(8,128)(2,1)} %get-tuple-element.8) | data formatting | bytes 2097152
  44.6 0.0 copy-done
  44.6 0.5 %copy.13 = f32[64]{0:T(128)} copy(f32[64]{0:T(128)S(1)} %bitcast.5) | data formatting | bytes 512
Async XLA Ops:
  42.3 2.3 %copy-start = (f32[1,64]{1,0:T(1,128)S(1)}, f32[1,64]{1,0:T(1,128)}, u32[]{:S(2)}) copy-start(f32[1,64]{1,0:T(1,128)} %get-tuple-element.5) | copy-start | bytes 772
